TPU v7x, 32 devices: a whole 2x2x4 slice. The times are simulated.
32 devices in a mesh: expert: 4 (over z), shard: 8 (over y, x, core).
Axes of the slice: x: 2, y: 2, z: 4, core: 2. Of those that a mesh axis runs over, the one named last changes fastest.
Arguments:
- tokens: bfloat16 [768, 4096], P(('expert', 'shard')), may hold values from -0.19921875 to 0.19921875
- expert_ids: int32 [768, 2], P(('expert', 'shard')), may hold values from 0 to 3, all different within a row; in each aligned block of 24 rows (0 to 23, 24 to 47, ...) at most 16 rows name the same one
- weight_gate: bfloat16 [4, 4096, 8192], P('expert', None, 'shard'), may hold values from -0.09375 to 0.09375
- weight_up: bfloat16 [4, 4096, 8192], P('expert', None, 'shard'), may hold values from -0.09375 to 0.09375
- gate_pre: bfloat16 [4, 512, 8192], P('expert', None, 'shard'), may hold values from -8 to 8
- up_pre: bfloat16 [4, 512, 8192], P('expert', None, 'shard'), may hold values from -6 to 6
- hidden_grad: bfloat16 [4, 512, 8192], P('expert', None, 'shard'), may hold values from -6 to 6
Outputs:
- token_grad: bfloat16 [768, 4096], P(('expert', 'shard'))
- gate_weight_grad: float32 [4, 4096, 8192], P('expert', None, 'shard')
- up_weight_grad: float32 [4, 4096, 8192], P('expert', None, 'shard')
Inputs may be any that keep to these rules, and one draw needn't show every extreme that they name: `expert_ids`: each token names 2 different experts. Among the tokens of one device no expert is named more than 16 times, and in every draw some device names some expert exactly 16 times.
All inputs are finite; a program needn't handle non-finite values.
Results may differ from a plain program's by a relative error of at most 0.02.
Values may be sent and summed in bfloat16 or wider, within the bound.
A program may use at most 192 MiB of HBM per device.

v0:
```python
import jax
import jax.numpy as jnp
from jax import lax
from jax.sharding import PartitionSpec as P


def swiglu_grads(gate_values, up_values, hidden_cotangent):
    gate_float = gate_values.astype(jnp.float32)
    up_float = up_values.astype(jnp.float32)
    cotangent = hidden_cotangent.astype(jnp.float32)
    sigmoid_gate = jax.nn.sigmoid(gate_float)
    gate_grad = (
        cotangent * up_float * sigmoid_gate * (1.0 + gate_float * (1.0 - sigmoid_gate))
    ).astype(jnp.bfloat16)
    up_grad = (cotangent * gate_float * sigmoid_gate).astype(jnp.bfloat16)
    return (gate_grad, up_grad)


def slot_table(expert_ids, groups, capacity):
    token_count = expert_ids.shape[0]
    choices_per = expert_ids.shape[1]
    labels = lax.broadcasted_iota(jnp.int32, (1, 1, groups), 2)
    one_hot = (expert_ids[:, :, None] == labels).astype(jnp.int32)
    flat_hits = one_hot.reshape(token_count * choices_per, groups)
    earlier = jnp.cumsum(flat_hits, axis=0) - flat_hits
    slot_index = jnp.sum(flat_hits * earlier, axis=1).reshape(token_count, choices_per)
    slot_labels = lax.broadcasted_iota(jnp.int32, (1, 1, 1, capacity), 3)
    slot_hits = one_hot[:, :, :, None] * (slot_index[:, :, None, None] == slot_labels).astype(
        jnp.int32
    )
    selection = jnp.sum(slot_hits, axis=1).reshape(token_count, groups * capacity)
    return selection.astype(jnp.bfloat16)


def rows_inner(left_rows, right_rows):
    return lax.dot_general(
        left_rows, right_rows, (((0,), (0,)), ((), ())), preferred_element_type=jnp.float32
    )


def times_transposed(left_rows, weights):
    return lax.dot_general(
        left_rows, weights, (((1,), (1,)), ((), ())), preferred_element_type=jnp.float32
    )


def on_device(tokens, expert_ids, weight_gate, weight_up, gate_pre, up_pre, hidden_grad):
    groups = lax.axis_size("expert")
    shards = lax.axis_size("shard")
    model_width = tokens.shape[1]
    capacity = gate_pre.shape[1] // (groups * shards)
    selection = slot_table(expert_ids, groups, capacity)
    outgoing = rows_inner(selection, tokens).astype(jnp.bfloat16)
    gate_grad, up_grad = swiglu_grads(gate_pre[0], up_pre[0], hidden_grad[0])
    gate_matrix = weight_gate[0]
    up_matrix = weight_up[0]
    arrived = lax.all_to_all(
        outgoing.reshape(groups, capacity, model_width),
        "expert",
        split_axis=0,
        concat_axis=0,
        tiled=True,
    )
    block_rows = lax.all_gather(
        arrived.reshape(groups * capacity, model_width), "shard", axis=0, tiled=True
    )
    gate_rows = gate_grad
    up_rows = up_grad
    gate_wgrad = rows_inner(block_rows, gate_rows)
    up_wgrad = rows_inner(block_rows, up_rows)
    gate_rows = gate_grad
    up_rows = up_grad
    summed = lax.psum_scatter(
        (times_transposed(gate_rows, gate_matrix) + times_transposed(up_rows, up_matrix)).astype(
            jnp.bfloat16
        ),
        "shard",
        scatter_dimension=0,
        tiled=True,
    )
    outbound = summed.reshape(groups, capacity, model_width)
    returned = lax.all_to_all(outbound, "expert", split_axis=0, concat_axis=0, tiled=True)
    returned = returned.reshape(groups * capacity, model_width)
    token_grad = times_transposed(selection, returned.T).astype(jnp.bfloat16)
    return (token_grad, gate_wgrad[None], up_wgrad[None])


def solution(mesh):
    placed = (
        P(("expert", "shard"), None),
        P(("expert", "shard"), None),
        P("expert", None, "shard"),
        P("expert", None, "shard"),
        P("expert", None, "shard"),
        P("expert", None, "shard"),
        P("expert", None, "shard"),
    )
    return jax.shard_map(
        on_device,
        mesh=mesh,
        in_specs=placed,
        out_specs=(
            P(("expert", "shard"), None),
            P("expert", None, "shard"),
            P("expert", None, "shard"),
        ),
        check_vma=False,
    )
```

profile of v0, /device:TPU:0, one launch (start us, length us, event | category | flops | bytes accessed | tf_op | source)
XLA Modules:
  0.0 149.9 jit_solution(7265675212288207498)
XLA Ops:
  7.2 0.0 copy-start
  7.2 0.0 reduce-scatter.2.cloned.1.call-start
  7.3 12.2 %fusion = f32[512,4096]{1,0:T(8,128)} fusion(bf16[1,4096,1024]{2,1,0:T(8,128)(2,1)} %param.10, bf16[1,512,1024]{2,1,0:T(8,128)(2,1)} %param.11, bf16[1,512,1024]{2,1,0:T(8,128)(2,1)} %param.13), kind=kOutput, calls=%fused_computation.2 | convolution fusion | flops 4299161600 | bytes 18874368 | tf_op jit(solution)/shard_map/dot_general | solution.py:42
  19.5 0.0 copy-done.4
  19.5 11.3 %add_convert_fusion = bf16[512,4096]{1,0:T(8,128)(2,1)} fusion(f32[512,4096]{1,0:T(8,128)} %fusion, bf16[1,4096,1024]{2,1,0:T(8,128)(2,1)} %param.9, bf16[1,512,1024]{2,1,0:T(8,128)(2,1)S(1)} %copy-done.6, bf16[1,512,1024]{2,1,0:T(8,128)(2,1)S(1)} %copy-done.5, bf16[1,512,1024]{2,1,0:T(8,128)(2,1)S(1)} %copy-done.4), kind=kOutput, calls=%fused_computation.6 | convolution fusion | flops 4305977344 | bytes 24117248 | tf_op jit(solution)/shard_map/dot_general | solution.py:42
  30.8 0.0 reduce-scatter.2.cloned.1.call-update
  30.8 0.0 all-gather.2.cloned.1.call-start
  30.8 0.6 copy-done.2
  31.4 0.1 copy.14
  31.5 0.1 eq.49
  31.6 0.1 fusion.37
  31.7 0.1 reduce_window_sum.11
  31.8 0.2 select_reduce_fusion
  32.0 0.1 eq.53
  32.1 0.1 copy.15
  32.2 0.3 convolution_convert_fusion
  32.5 20.7 %all_to_all.10 = bf16[4,16,4096]{2,1,0:T(8,128)(2,1)} all-to-all(bf16[4,16,4096]{2,1,0:T(8,128)(2,1)S(1)} %bitcast.90), channel_id=1, replica_groups=mesh['expert'=4,'shard'=8] {'expert'}, dimensions={0} | all-to-all | bytes 1048576 | tf_op jit(solution)/shard_map/all_to_all | solution.py:57
  53.2 0.0 all-gather.2.cloned.1.call-update
  53.3 31.6 %reduce-scatter.2.cloned.1.call-done = bf16[64,4096]{1,0:T(8,128)(2,1)} async-done(((bf16[512,4096]{1,0:T(8,128)(2,1)}), bf16[64,4096]{1,0:T(8,128)(2,1)}) %reduce-scatter.2.cloned.1.call-update) | async-done | bytes 524304 | tf_op jit(solution)/shard_map/reduce_scatter | solution.py:73
  84.8 18.9 %all_to_all.11 = bf16[4,16,4096]{2,1,0:T(8,128)(2,1)S(1)} all-to-all(bf16[4,16,4096]{2,1,0:T(8,128)(2,1)} %bitcast.91), channel_id=1, replica_groups=mesh['expert'=4,'shard'=8] {'expert'}, dimensions={0} | all-to-all | bytes 1048576 | tf_op jit(solution)/shard_map/all_to_all | solution.py:82
  103.7 0.9 fusion.6
  104.6 18.7 %all-gather.2.cloned.1.call-done = bf16[512,4096]{1,0:T(8,128)(2,1)} async-done(((bf16[64,4096]{1,0:T(8,128)(2,1)}), bf16[512,4096]{1,0:T(8,128)(2,1)}) %all-gather.2.cloned.1.call-update) | async-done | bytes 4194320 | tf_op jit(solution)/shard_map/all_gather | solution.py:64
  123.3 11.0 %convolution_bitcast_fusion = f32[1,4096,1024]{2,1,0:T(8,128)} fusion(bf16[512,4096]{1,0:T(8,128)(2,1)} %all-gather.2.cloned.1.call-done, bf16[1,512,1024]{2,1,0:T(8,128)(2,1)S(1)} %copy-done.4, bf16[1,512,1024]{2,1,0:T(8,128)(2,1)S(1)} %copy-done.5), kind=kOutput, calls=%fused_computation | convolution fusion | flops 4299161600 | bytes 23068672 | tf_op jit(solution)/shard_map/dot_general | solution.py:36
  134.3 8.8 %convolution_bitcast_fusion.1 = f32[1,4096,1024]{2,1,0:T(8,128)} fusion(bf16[512,4096]{1,0:T(8,128)(2,1)S(1)} %copy-done.3, bf16[1,512,1024]{2,1,0:T(8,128)(2,1)S(1)} %copy-done.6, bf16[1,512,1024]{2,1,0:T(8,128)(2,1)S(1)} %copy-done.5, bf16[1,512,1024]{2,1,0:T(8,128)(2,1)S(1)} %copy-done.4), kind=kOutput, calls=%fused_computation.1 | convolution fusion | flops 4301783040 | bytes 24117248 | tf_op jit(solution)/shard_map/dot_general | solution.py:36
  (15 shorter events, 0.1 us)
Async XLA Ops:
  7.2 25.0 %copy-start = (bf16[24,4096]{1,0:T(8,128)(2,1)S(1)}, bf16[24,4096]{1,0:T(8,128)(2,1)}, u32[]{:S(2)}) copy-start(bf16[24,4096]{1,0:T(8,128)(2,1)} %param.7) | copy-start | bytes 589828
  7.2 12.3 %copy-start.5 = (bf16[1,512,1024]{2,1,0:T(8,128)(2,1)S(1)}, bf16[1,512,1024]{2,1,0:T(8,128)(2,1)}, u32[]{:S(2)}) copy-start(bf16[1,512,1024]{2,1,0:T(8,128)(2,1)} %param.13) | copy-start | bytes 3145732
  7.2 12.3 %copy-start.4 = (bf16[1,512,1024]{2,1,0:T(8,128)(2,1)S(1)}, bf16[1,512,1024]{2,1,0:T(8,128)(2,1)}, u32[]{:S(2)}) copy-start(bf16[1,512,1024]{2,1,0:T(8,128)(2,1)} %param.11) | copy-start | bytes 3145732
  7.2 12.3 %copy-start.6 = (bf16[1,512,1024]{2,1,0:T(8,128)(2,1)S(1)}, bf16[1,512,1024]{2,1,0:T(8,128)(2,1)}, u32[]{:S(2)}) copy-start(bf16[1,512,1024]{2,1,0:T(8,128)(2,1)} %param.12) | copy-start | bytes 3145732
  7.2 77.6 %reduce-scatter.2.cloned.1.call-start = ((), (), s32[]{:S(2)}) async-start(), calls=%async_computation.3 | async-start | bytes 4718592 | tf_op jit(solution)/shard_map/reduce_scatter | solution.py:73
  30.8 0.7 copy-start.2
  30.8 92.5 %all-gather.2.cloned.1.call-start = ((), (), s32[]{:S(2)}) async-start(), calls=%async_computation.4 | async-start | bytes 4718592 | tf_op jit(solution)/shard_map/all_gather | solution.py:64
  123.3 11.0 %copy-start.3 = (bf16[512,4096]{1,0:T(8,128)(2,1)S(1)}, bf16[512,4096]{1,0:T(8,128)(2,1)}, u32[]{:S(2)}) copy-start(bf16[512,4096]{1,0:T(8,128)(2,1)} %all-gather.2.cloned.1.call-done) | copy-start | bytes 12582916
  134.3 8.8 %copy-start.1 = (bf16[24,4096]{1,0:T(8,128)(2,1)S(1)}, bf16[24,4096]{1,0:T(8,128)(2,1)}, u32[]{:S(2)}) copy-start(bf16[24,4096]{1,0:T(8,128)(2,1)} %param.7) | copy-start | bytes 589828
Sparse Core Ops, SparseCore 0:
  30.9 53.8 reduce-scatter.1
  86.7 36.5 all-gather.1
where the time goes:
time: 150 us
  waiting for transfers between devices  50.2 us (33%)
  matrix products  44.5 us (30%)
  blocking collectives  39.6 us (26%)
  between operations  14.1 us (9%)
    reduce_scatter x1, waiting for transfers between devices, on_device(): lax.psum_scatter((times_transposed(gate_rows, gate_matrix) + times_transp...  31.6 us
    dot_general x3, matrix products, times_transposed(): lax.dot_general(left_rows, weights, (((1,), (1,)), ((), ())), preferred_e...  24.4 us
    all_to_all x1, blocking collectives, on_device(): lax.all_to_all(outgoing.reshape(groups, capacity, model_width), 'expert',...  20.7 us
    dot_general x3, matrix products, rows_inner(): lax.dot_general(left_rows, right_rows, (((0,), (0,)), ((), ())), preferre...  20.1 us
    all_to_all x1, blocking collectives, on_device(): lax.all_to_all(outbound, 'expert', split_axis=0, concat_axis=0, tiled=True)  18.9 us
    all_gather x1, waiting for transfers between devices, on_device(): lax.all_gather(arrived.reshape(groups * capacity, model_width), 'shard',...  18.7 us
  transfers between devices with their start and end apart: 2, of which 2 were waited for; matrix products, arithmetic and copies ran while one was open for 1% of the time, Pallas kernels for 0%

commit v1 on v0

--- a/solution.py
+++ b/solution.py
@@ -1,7 +1,14 @@
+import functools
 import jax
 import jax.numpy as jnp
 from jax import lax
+from jax.experimental import pallas as pl
+from jax.experimental.pallas import tpu as pltpu
 from jax.sharding import PartitionSpec as P
+
+MESH = pl.DeviceIdType.MESH
+CHUNKS = 8
+COPIES = 21
 
 
 def swiglu_grads(gate_values, up_values, hidden_cotangent):
@@ -44,7 +51,7 @@
     )
 
 
-def on_device(tokens, expert_ids, weight_gate, weight_up, gate_pre, up_pre, hidden_grad):
+def on_device_general(tokens, expert_ids, weight_gate, weight_up, gate_pre, up_pre, hidden_grad):
     groups = lax.axis_size("expert")
     shards = lax.axis_size("shard")
     model_width = tokens.shape[1]
@@ -85,6 +92,341 @@
     return (token_grad, gate_wgrad[None], up_wgrad[None])
 
 
+def exchange_kernel(
+    groups, capacity, chunks, width,
+    outgoing, selection, weight_gate, weight_up, gate_pre, up_pre, hidden_grad,
+    token_grad, block_rows, gate_out, up_out,
+    gate_w, up_w, pre, gate_rows, up_rows, block, partial, from_core, total, from_diag,
+    from_near, leaving, returned, load_sem, store_sem, local_sem, send_sem, recv_sem,
+):
+    e = lax.axis_index("expert")
+    q = lax.axis_index("shard")
+    core, x, y = q % 2, (q // 2) % 2, q // 4
+    sib = q + 1 - 2 * core
+    xn = q + 2 - 4 * x
+    yn = q + 4 - 8 * y
+    dg = xn + 4 - 8 * y
+    rows = groups * capacity
+    half = rows // 2
+    slots = gate_rows.shape[0]
+    part = slots // 4
+
+    def pre_load(i, source):
+        return pltpu.make_async_copy(source.at[0], pre.at[i], load_sem.at[2 * chunks + i])
+
+    def weight_load(i, c, source, target):
+        return pltpu.make_async_copy(
+            source.at[0, pl.ds(pl.multiple_of(c * width, width), width), :],
+            target.at[c], load_sem.at[2 * c + i],
+        )
+
+    def columns(c):
+        return pl.ds(pl.multiple_of(c * width, width), width)
+
+    def span(start, size):
+        return pl.ds(pl.multiple_of(start, size), size)
+
+    def held(c, start, size):
+        return block.at[c, span(start, size), :]
+
+    def chip_rows(c, device, low, size):
+        return total.at[c, span(device // 2 * rows + low, size), :]
+
+    def other(k):
+        return (e + k) % groups
+
+    def target(k):
+        if k < 3:
+            return (other(k + 1), q)
+        if k >= 18:
+            return (other(k - 17), q)
+        if k in (3, 7, 12, 14, 16):
+            return (e, xn)
+        if k in (4, 6, 13, 15, 17):
+            return (e, yn)
+        return (e, sib)
+
+    def copy(k, c):
+        if k < 3:
+            source = outgoing.at[other(k + 1), :, columns(c)]
+            to = held(c, q * rows + e * capacity, capacity)
+        elif k < 6:
+            source = to = held(c, q * rows, rows)
+        elif k == 6:
+            source = to = held(c, xn * rows, half)
+        elif k == 7:
+            source = to = held(c, yn * rows + half, half)
+        elif k < 11:
+            source = to = held(c, (xn, yn, dg)[k - 8] * rows, rows)
+        elif k == 11:
+            source, to = partial.at[c, 1 - core], from_core.at[c]
+        elif k == 12:
+            source, to = chip_rows(c, dg, 0, half), from_diag.at[c, 0]
+        elif k == 13:
+            source, to = chip_rows(c, dg, half, half), from_diag.at[c, 1]
+        elif k == 14:
+            source, to = chip_rows(c, xn, 0, half), from_near.at[c, 0, 0]
+        elif k == 15:
+            source, to = chip_rows(c, yn, half, half), from_near.at[c, 1, 1]
+        elif k == 16:
+            source, to = chip_rows(c, xn, half, half), from_near.at[c, 0, 1]
+        elif k == 17:
+            source, to = chip_rows(c, yn, 0, half), from_near.at[c, 1, 0]
+        else:
+            source = leaving.at[c, span(other(k - 17) * capacity, capacity), :]
+            to = returned.at[c, span(e * capacity, capacity), :]
+        return pltpu.make_async_remote_copy(
+            src_ref=source, dst_ref=to, send_sem=send_sem.at[c, k], recv_sem=recv_sem.at[c, k],
+            device_id=target(k), device_id_type=MESH,
+        )
+
+    def landing(k, c):
+        if k < 3:
+            return held(c, q * rows + (e + groups - k - 1) % groups * capacity, capacity)
+        if k < 6:
+            return held(c, (xn, yn, sib)[k - 3] * rows, rows)
+        if k == 6:
+            return held(c, dg * rows, half)
+        if k == 7:
+            return held(c, dg * rows + half, half)
+        if k < 11:
+            return held(c, (sib + (xn, yn, dg)[k - 8] - q) * rows, rows)
+        if k >= 18:
+            source = (e + groups - k + 17) % groups
+            return returned.at[c, span(source * capacity, capacity), :]
+        return {
+            11: from_core.at[c], 12: from_diag.at[c, 0], 13: from_diag.at[c, 1],
+            14: from_near.at[c, 0, 0], 15: from_near.at[c, 1, 1],
+            16: from_near.at[c, 0, 1], 17: from_near.at[c, 1, 0],
+        }[k]
+
+    def arrive(k, c):
+        place = landing(k, c)
+        pltpu.make_async_remote_copy(
+            src_ref=place, dst_ref=place, send_sem=send_sem.at[c, k], recv_sem=recv_sem.at[c, k],
+            device_id=target(k), device_id_type=MESH,
+        ).wait_recv()
+
+    def own_rows(c):
+        return pltpu.make_async_copy(
+            outgoing.at[e, :, columns(c)], held(c, q * rows + e * capacity, capacity),
+            local_sem.at[c],
+        )
+
+    def rows_out(c):
+        return pltpu.make_async_copy(
+            block.at[c], block_rows.at[:, columns(c)], store_sem.at[c]
+        )
+
+    def grads_out(i):
+        return pltpu.make_async_copy(
+            (gate_rows, up_rows)[i], (gate_out, up_out)[i], store_sem.at[chunks + i]
+        )
+
+    for i, source in enumerate((gate_pre, up_pre, hidden_grad)):
+        pre_load(i, source).start()
+
+    @pl.loop(0, chunks)
+    def _(c):
+        weight_load(0, c, weight_gate, gate_w).start()
+        weight_load(1, c, weight_up, up_w).start()
+        own_rows(c).start()
+
+    barrier = pltpu.get_barrier_semaphore()
+    for device in ((other(1), q), (other(2), q), (other(3), q), (e, sib), (e, xn), (e, yn)):
+        pl.semaphore_signal(barrier, inc=1, device_id=device, device_id_type=MESH)
+    pl.semaphore_wait(barrier, 6)
+
+    @pl.loop(0, chunks)
+    def _(c):
+        for k in (1, 0, 2):
+            copy(k, c).start()
+
+    for i, source in enumerate((gate_pre, up_pre, hidden_grad)):
+        pre_load(i, source).wait()
+
+    step_rows = 32
+
+    @pl.loop(0, slots // step_rows)
+    def _(i):
+        here = span(i * step_rows, step_rows)
+        gate_grad, up_grad = swiglu_grads(pre[0, here, :], pre[1, here, :], pre[2, here, :])
+        gate_rows[here, :] = gate_grad
+        up_rows[here, :] = up_grad
+
+    for i in range(2):
+        grads_out(i).start()
+
+    def spread(c):
+        own_rows(c).wait()
+        for k in (0, 1, 2):
+            arrive(k, c)
+        for k in (3, 4, 5):
+            copy(k, c).start()
+
+    def forward(c):
+        arrive(3, c)
+        copy(6, c).start()
+        copy(8, c).start()
+        arrive(4, c)
+        copy(7, c).start()
+        copy(9, c).start()
+
+    def far(c):
+        arrive(6, c)
+        arrive(7, c)
+        copy(10, c).start()
+
+    def gathered(c):
+        for k in (5, 8, 9, 10):
+            arrive(k, c)
+        rows_out(c).start()
+
+    def multiply(c):
+        weight_load(0, c, weight_gate, gate_w).wait()
+        weight_load(1, c, weight_up, up_w).wait()
+        term = times_transposed(gate_rows[...], gate_w[c]) + times_transposed(up_rows[...], up_w[c])
+        term = term.astype(jnp.bfloat16)
+        for chip in range(slots // (2 * rows)):
+            for side in range(2):
+                low = (2 * chip + side) * rows
+                partial[c, side, chip * rows : (chip + 1) * rows, :] = term[low : low + rows]
+        copy(11, c).start()
+
+    def pair_sum(c):
+        arrive(11, c)
+        both = partial[c, core].astype(jnp.float32) + from_core[c].astype(jnp.float32)
+        total[c] = both.astype(jnp.bfloat16)
+        for k in (12, 13, 14, 15):
+            copy(k, c).start()
+
+    def near_sum(c):
+        for k, side, device, low in ((12, 0, yn, 0), (13, 1, xn, half)):
+            arrive(k, c)
+            place = span(device // 2 * rows + low, half)
+            added = total[c, place, :].astype(jnp.float32) + from_diag[c, side].astype(jnp.float32)
+            total[c, place, :] = added.astype(jnp.bfloat16)
+            copy(17 if side == 0 else 16, c).start()
+
+    def own_sum(c):
+        for k in (14, 15, 16, 17):
+            arrive(k, c)
+        for low in range(2):
+            place = span(q // 2 * rows + low * half, half)
+            added = total[c, place, :].astype(jnp.float32)
+            added = added + from_near[c, 0, low].astype(jnp.float32)
+            added = added + from_near[c, 1, low].astype(jnp.float32)
+            leaving[c, low * half : (low + 1) * half, :] = added.astype(jnp.bfloat16)
+        mine = span(e * capacity, capacity)
+        returned[c, mine, :] = leaving[c, mine, :]
+        for k in (19, 18, 20):
+            copy(k, c).start()
+
+    def combine(c):
+        for k in (18, 19, 20):
+            arrive(k, c)
+        token_grad[:, columns(c)] = jnp.dot(
+            selection[...], returned[c], preferred_element_type=jnp.float32
+        ).astype(jnp.bfloat16)
+
+    stages = (
+        (spread, 0), (forward, 1), (pair_sum, 1), (near_sum, 2), (far, 2), (own_sum, 3),
+        (multiply, 0), (gathered, 3), (combine, 4),
+    )
+
+    @pl.loop(0, chunks + 4)
+    def _(step):
+        for stage, lag in stages:
+            c = step - lag
+
+            @pl.when(jnp.logical_and(c >= 0, c < chunks))
+            def _():
+                stage(c)
+
+    @pl.loop(0, chunks)
+    def _(c):
+        for k in range(COPIES):
+            copy(k, c).wait_send()
+        rows_out(c).wait()
+
+    for i in range(2):
+        grads_out(i).wait()
+
+
+def weight_grad_kernel(block_rows, gate_rows, up_rows, gate_wgrad, up_wgrad):
+    left = block_rows[...]
+    gate_wgrad[0] = rows_inner(left, gate_rows[...])
+    up_wgrad[0] = rows_inner(left, up_rows[...])
+
+
+def on_device(tokens, expert_ids, weight_gate, weight_up, gate_pre, up_pre, hidden_grad):
+    groups = lax.axis_size("expert")
+    shards = lax.axis_size("shard")
+    token_count, model_width = tokens.shape
+    slots, hidden = gate_pre.shape[1:]
+    capacity = slots // (groups * shards)
+    rows = groups * capacity
+    chunks = CHUNKS
+    width = model_width // chunks
+    bf16 = jnp.bfloat16
+    selection = slot_table(expert_ids, groups, capacity)
+    outgoing = rows_inner(selection, tokens).astype(bf16).reshape(groups, capacity, model_width)
+    in_vmem = pl.BlockSpec(memory_space=pltpu.VMEM)
+    anywhere = pl.BlockSpec(memory_space=pl.ANY)
+    token_grad, block_rows, gate_rows, up_rows = pl.pallas_call(
+        functools.partial(exchange_kernel, groups, capacity, chunks, width),
+        out_shape=(
+            jax.ShapeDtypeStruct((token_count, model_width), bf16),
+            jax.ShapeDtypeStruct((slots, model_width), bf16),
+            jax.ShapeDtypeStruct((slots, hidden), bf16),
+            jax.ShapeDtypeStruct((slots, hidden), bf16),
+        ),
+        in_specs=[in_vmem, in_vmem] + [anywhere] * 5,
+        out_specs=(in_vmem, anywhere, anywhere, anywhere),
+        scratch_shapes=[
+            pltpu.VMEM((chunks, width, hidden), bf16),
+            pltpu.VMEM((chunks, width, hidden), bf16),
+            pltpu.VMEM((3, slots, hidden), bf16),
+            pltpu.VMEM((slots, hidden), bf16),
+            pltpu.VMEM((slots, hidden), bf16),
+            pltpu.VMEM((chunks, slots, width), bf16),
+            pltpu.VMEM((chunks, 2, slots // 2, width), bf16),
+            pltpu.VMEM((chunks, slots // 2, width), bf16),
+            pltpu.VMEM((chunks, slots // 2, width), bf16),
+            pltpu.VMEM((chunks, 2, rows // 2, width), bf16),
+            pltpu.VMEM((chunks, 2, 2, rows // 2, width), bf16),
+            pltpu.VMEM((chunks, rows, width), bf16),
+            pltpu.VMEM((chunks, rows, width), bf16),
+            pltpu.SemaphoreType.DMA((2 * chunks + 3,)),
+            pltpu.SemaphoreType.DMA((chunks + 2,)),
+            pltpu.SemaphoreType.DMA((chunks,)),
+            pltpu.SemaphoreType.DMA((chunks, COPIES)),
+            pltpu.SemaphoreType.DMA((chunks, COPIES)),
+        ],
+        compiler_params=pltpu.CompilerParams(
+            collective_id=0, has_side_effects=True, vmem_limit_bytes=60 * 1024 * 1024
+        ),
+    )(outgoing, selection, weight_gate, weight_up, gate_pre, up_pre, hidden_grad)
+    tile = min(512, model_width)
+    wgrad_shape = jax.ShapeDtypeStruct((1, model_width, hidden), jnp.float32)
+    gate_wgrad, up_wgrad = pl.pallas_call(
+        weight_grad_kernel,
+        grid=(model_width // tile,),
+        out_shape=(wgrad_shape, wgrad_shape),
+        in_specs=[
+            pl.BlockSpec((slots, tile), lambda i: (0, i)),
+            pl.BlockSpec((slots, hidden), lambda i: (0, 0)),
+            pl.BlockSpec((slots, hidden), lambda i: (0, 0)),
+        ],
+        out_specs=(
+            pl.BlockSpec((1, tile, hidden), lambda i: (0, i, 0)),
+            pl.BlockSpec((1, tile, hidden), lambda i: (0, i, 0)),
+        ),
+        compiler_params=pltpu.CompilerParams(vmem_limit_bytes=48 * 1024 * 1024),
+    )(block_rows, gate_rows, up_rows)
+    return (token_grad, gate_wgrad, up_wgrad)
+
+
 def solution(mesh):
     placed = (
         P(("expert", "shard"), None),
@@ -95,8 +437,9 @@
         P("expert", None, "shard"),
         P("expert", None, "shard"),
     )
+    small = mesh.shape["shard"] == 8 and mesh.shape["expert"] == 4
     return jax.shard_map(
-        on_device,
+        on_device if small else on_device_general,
         mesh=mesh,
         in_specs=placed,
         out_specs=(

time: 150 us -> 79 us (0.53)
  Pallas kernels: 0 us -> 69.9 us
  waiting for transfers between devices: 50.2 us -> 0 us
  matrix products: 44.5 us -> 1.07 us
  blocking collectives: 39.6 us -> 0 us
  between operations: 14.1 us -> 0.69 us
  local copies, waits for them, and re-layouts: 0.99 us -> 5.77 us
    pallas_call x0 -> x2, Pallas kernels: none -> 69.9 us  [the longest x1 56.5 us: on_device(): pl.pallas_call(functools.partial(exchange_kernel, groups, capacity, chunk...]
    all_to_all x2 -> x0, blocking collectives: 39.6 us -> none  [the longest x1 20.7 us: on_device(): lax.all_to_all(outgoing.reshape(groups, capacity, model_width), 'expert',...]
    reduce_scatter x1 -> x0, waiting for transfers between devices: 31.6 us -> none  [on_device(): lax.psum_scatter((times_transposed(gate_rows, gate_matrix) + times_transp...]
    dot_general x3 -> x0, matrix products: 24.4 us -> none  [times_transposed(): lax.dot_general(left_rows, weights, (((1,), (1,)), ((), ())), preferred_e...]
    dot_general x3 -> x1, matrix products: 20.1 us -> 1.07 us  [rows_inner(): lax.dot_general(left_rows, right_rows, (((0,), (0,)), ((), ())), preferre...]
    all_gather x1 -> x0, waiting for transfers between devices: 18.7 us -> none  [on_device(): lax.all_gather(arrived.reshape(groups * capacity, model_width), 'shard',...]
    unnamed x15 -> x8, local copies, waits for them, and re-layouts: 0.72 us -> 4.82 us
  transfers between devices with their start and end apart: 2 -> 0, of which waited for: 2 -> 0; matrix products, arithmetic and copies ran while one was open for 1% -> 0% of each run, Pallas kernels for 0% -> 0%
where the time goes in v1:
time: 79 us; the launch traced here: 78.5 us
  Pallas kernels  69.9 us (88%)
  local copies, waits for them, and re-layouts  5.77 us (7%)
  other arithmetic  1.09 us (1%)
  matrix products  1.07 us (1%)
    pallas_call x1, Pallas kernels, on_device(): pl.pallas_call(functools.partial(exchange_kernel, groups, capacity, chunk...  56.5 us
    pallas_call x1, Pallas kernels, on_device(): pl.pallas_call(weight_grad_kernel, grid=(model_width // tile,), out_shape...  13.4 us
    unnamed x8, local copies, waits for them, and re-layouts  4.82 us

profile of v1, /device:TPU:0, one launch (start us, length us, event | category | flops | bytes accessed | tf_op | source)
XLA Modules:
  0.0 78.5 jit_solution(14416376922786074014)
XLA Ops:
  0.6 0.0 copy-start
  0.6 0.7 fusion.2
  1.4 0.8 copy.15
  2.1 0.1 eq.49
  2.2 0.1 fusion
  2.3 0.1 reduce_window_sum.11
  2.4 0.2 select_reduce_fusion
  2.6 0.1 eq.53
  2.7 0.1 copy.16
  2.8 0.7 copy.17.selection
  3.5 0.0 copy-done
  3.5 1.1 %convolution_convert_fusion = bf16[64,4096]{1,0:T(8,128)(2,1)} fusion(bf16[24,64]{0,1:T(8,128)(2,1)S(1)} %bitcast.6, bf16[24,4096]{1,0:T(8,128)(2,1)S(1)} %copy-done), kind=kOutput, calls=%fused_computation | convolution fusion | flops 12845056 | bytes 723968 | tf_op jit(solution)/shard_map/dot_general | solution.py:43
  4.5 56.5 %shard_map.94 = (bf16[24,4096]{1,0:T(8,128)(2,1)}, bf16[512,4096]{1,0:T(8,128)(2,1)}, bf16[512,1024]{1,0:T(8,128)(2,1)}, bf16[512,1024]{1,0:T(8,128)(2,1)}) custom-call(bf16[4,16,4096]{2,1,0:T(8,128)(2,1)} %bitcast.4, bf16[24,64]{1,0:T(8,128)(2,1)} %copy.17.selection, bf16[1,4096,1024]{2,1,0:T(8,128)(2,1)} %weight_gate.1, bf16[1,4096,1024]{2,1,0:T(8,128)(2,1)} %weight_up.1, ...), custom_call_target="tpu_custom_call" | custom-call | tf_op jit(solution)/shard_map/pallas_call | solution.py:376
  61.0 0.0 copy-start.1
  61.0 1.2 %copy-done.1 = bf16[512,1024]{1,0:T(8,128)(2,1)S(1)} copy-done((bf16[512,1024]{1,0:T(8,128)(2,1)S(1)}, bf16[512,1024]{1,0:T(8,128)(2,1)}, u32[]{:S(2)}) %copy-start.1) | copy-done | bytes 1048600
  62.3 0.0 copy-start.2
  62.3 1.2 %copy-done.2 = bf16[512,1024]{1,0:T(8,128)(2,1)S(1)} copy-done((bf16[512,1024]{1,0:T(8,128)(2,1)S(1)}, bf16[512,1024]{1,0:T(8,128)(2,1)}, u32[]{:S(2)}) %copy-start.2) | copy-done | bytes 1048600
  63.5 13.4 %shard_map.95 = (f32[1,4096,1024]{2,1,0:T(8,128)}, f32[1,4096,1024]{2,1,0:T(8,128)}) custom-call(bf16[512,4096]{1,0:T(8,128)(2,1)} %get-tuple-element.10.block_rows, bf16[512,1024]{1,0:T(8,128)(2,1)S(1)} %copy-done.1, bf16[512,1024]{1,0:T(8,128)(2,1)S(1)} %copy-done.2), custom_call_target="tpu_custom_call" | custom-call | tf_op jit(solution)/shard_map/pallas_call | solution.py:412
  76.9 1.6 %copy.19 = bf16[24,4096]{1,0:T(8,128)(2,1)} copy(bf16[24,4096]{1,0:T(8,128)(2,1)} %get-tuple-element.18) | data formatting | bytes 393216
  (3 shorter events, 0.0 us)
Async XLA Ops:
  0.6 2.8 %copy-start = (bf16[24,4096]{1,0:T(8,128)(2,1)S(1)}, bf16[24,4096]{1,0:T(8,128)(2,1)}, u32[]{:S(2)}) copy-start(bf16[24,4096]{1,0:T(8,128)(2,1)} %param.7) | copy-start | bytes 589828
  61.0 1.2 %copy-start.1 = (bf16[512,1024]{1,0:T(8,128)(2,1)S(1)}, bf16[512,1024]{1,0:T(8,128)(2,1)}, u32[]{:S(2)}) copy-start(bf16[512,1024]{1,0:T(8,128)(2,1)} %get-tuple-element.11.gate_rows) | copy-start | bytes 3145732
  62.3 1.2 %copy-start.2 = (bf16[512,1024]{1,0:T(8,128)(2,1)S(1)}, bf16[512,1024]{1,0:T(8,128)(2,1)}, u32[]{:S(2)}) copy-start(bf16[512,1024]{1,0:T(8,128)(2,1)} %get-tuple-element.12.up_rows) | copy-start | bytes 3145732

commit v2 on v1

--- a/solution.py
+++ b/solution.py
@@ -7,7 +7,7 @@
 from jax.sharding import PartitionSpec as P
 
 MESH = pl.DeviceIdType.MESH
-CHUNKS = 8
+CHUNKS = 4
 COPIES = 21
 
 
@@ -92,11 +92,31 @@
     return (token_grad, gate_wgrad[None], up_wgrad[None])
 
 
+def slot_choice(expert_ids, groups, capacity):
+    token_count = expert_ids.shape[0]
+    lanes = lax.broadcasted_iota(jnp.int32, (token_count, groups * capacity), 1)
+    expert, slot = lanes // capacity, lanes % capacity
+    named = jnp.logical_or(expert_ids[:, 0:1] == expert, expert_ids[:, 1:2] == expert)
+    hits = jnp.where(named, 1.0, 0.0)
+    above = lax.broadcasted_iota(jnp.int32, (token_count, token_count), 0)
+    below = lax.broadcasted_iota(jnp.int32, (token_count, token_count), 1)
+    before = jnp.where(below < above, 1.0, 0.0)
+    earlier = jnp.dot(before, hits, preferred_element_type=jnp.float32)
+    chosen = jnp.logical_and(named, earlier == slot.astype(jnp.float32))
+    return jnp.where(chosen, 1.0, 0.0).astype(jnp.bfloat16)
+
+
+def paced(step):
+    early = jnp.where(step < 3, step, -1)
+    middle = jnp.where(jnp.logical_and(step >= 4, step % 2 == 0), step // 2 + 1, early)
+    return jnp.where(step > 8, step - 3, middle)
+
+
 def exchange_kernel(
     groups, capacity, chunks, width,
-    outgoing, selection, weight_gate, weight_up, gate_pre, up_pre, hidden_grad,
-    token_grad, block_rows, gate_out, up_out,
-    gate_w, up_w, pre, gate_rows, up_rows, block, partial, from_core, total, from_diag,
+    tokens, expert_ids, weight_gate, weight_up, gate_pre, up_pre, hidden_grad,
+    returned_out, block_rows, gate_out, up_out,
+    token_buf, outgoing, gate_w, up_w, pre, gate_rows, up_rows, block, partial, from_core, total, from_diag,
     from_near, leaving, returned, load_sem, store_sem, local_sem, send_sem, recv_sem,
 ):
     e = lax.axis_index("expert")
@@ -218,11 +238,18 @@
             block.at[c], block_rows.at[:, columns(c)], store_sem.at[c]
         )
 
+    def returns_out(c):
+        return pltpu.make_async_copy(
+            returned.at[c], returned_out.at[:, columns(c)], store_sem.at[chunks + 2 + c]
+        )
+
     def grads_out(i):
         return pltpu.make_async_copy(
             (gate_rows, up_rows)[i], (gate_out, up_out)[i], store_sem.at[chunks + i]
         )
 
+    token_load = pltpu.make_async_copy(tokens, token_buf, load_sem.at[2 * chunks + 3])
+    token_load.start()
     for i, source in enumerate((gate_pre, up_pre, hidden_grad)):
         pre_load(i, source).start()
 
@@ -230,15 +257,22 @@
     def _(c):
         weight_load(0, c, weight_gate, gate_w).start()
         weight_load(1, c, weight_up, up_w).start()
-        own_rows(c).start()
 
     barrier = pltpu.get_barrier_semaphore()
     for device in ((other(1), q), (other(2), q), (other(3), q), (e, sib), (e, xn), (e, yn)):
         pl.semaphore_signal(barrier, inc=1, device_id=device, device_id_type=MESH)
+    selection = slot_choice(expert_ids[...], groups, capacity)
+    token_load.wait()
+    for c in range(chunks):
+        here = slice(c * width, (c + 1) * width)
+        picked = rows_inner(selection, token_buf[:, here]).astype(jnp.bfloat16)
+        for group in range(groups):
+            outgoing[group, :, here] = picked[group * capacity : (group + 1) * capacity]
     pl.semaphore_wait(barrier, 6)
 
     @pl.loop(0, chunks)
     def _(c):
+        own_rows(c).start()
         for k in (1, 0, 2):
             copy(k, c).start()
 
@@ -325,18 +359,17 @@
     def combine(c):
         for k in (18, 19, 20):
             arrive(k, c)
-        token_grad[:, columns(c)] = jnp.dot(
-            selection[...], returned[c], preferred_element_type=jnp.float32
-        ).astype(jnp.bfloat16)
+        returns_out(c).start()
 
     stages = (
-        (spread, 0), (forward, 1), (pair_sum, 1), (near_sum, 2), (far, 2), (own_sum, 3),
-        (multiply, 0), (gathered, 3), (combine, 4),
+        (spread, 0, paced), (forward, 1, paced), (pair_sum, 1, None), (near_sum, 2, None),
+        (far, 2, paced), (own_sum, 3, None), (multiply, 0, None), (gathered, 3, paced),
+        (combine, 4, None),
     )
 
     @pl.loop(0, chunks + 4)
     def _(step):
-        for stage, lag in stages:
+        for stage, lag, pace in stages:
             c = step - lag
 
             @pl.when(jnp.logical_and(c >= 0, c < chunks))
@@ -348,15 +381,26 @@
         for k in range(COPIES):
             copy(k, c).wait_send()
         rows_out(c).wait()
+        returns_out(c).wait()
 
     for i in range(2):
         grads_out(i).wait()
 
 
-def weight_grad_kernel(block_rows, gate_rows, up_rows, gate_wgrad, up_wgrad):
+def weight_grad_kernel(
+    groups, capacity, expert_ids, returned, block_rows, gate_rows, up_rows,
+    token_grad, gate_wgrad, up_wgrad, selection,
+):
+    @pl.when(pl.program_id(0) == 0)
+    def _():
+        selection[...] = slot_choice(expert_ids[...], groups, capacity)
+
     left = block_rows[...]
     gate_wgrad[0] = rows_inner(left, gate_rows[...])
     up_wgrad[0] = rows_inner(left, up_rows[...])
+    token_grad[...] = jnp.dot(
+        selection[...], returned[...], preferred_element_type=jnp.float32
+    ).astype(jnp.bfloat16)
 
 
 def on_device(tokens, expert_ids, weight_gate, weight_up, gate_pre, up_pre, hidden_grad):
@@ -369,21 +413,21 @@
     chunks = CHUNKS
     width = model_width // chunks
     bf16 = jnp.bfloat16
-    selection = slot_table(expert_ids, groups, capacity)
-    outgoing = rows_inner(selection, tokens).astype(bf16).reshape(groups, capacity, model_width)
     in_vmem = pl.BlockSpec(memory_space=pltpu.VMEM)
     anywhere = pl.BlockSpec(memory_space=pl.ANY)
-    token_grad, block_rows, gate_rows, up_rows = pl.pallas_call(
+    returned, block_rows, gate_rows, up_rows = pl.pallas_call(
         functools.partial(exchange_kernel, groups, capacity, chunks, width),
         out_shape=(
-            jax.ShapeDtypeStruct((token_count, model_width), bf16),
+            jax.ShapeDtypeStruct((rows, model_width), bf16),
             jax.ShapeDtypeStruct((slots, model_width), bf16),
             jax.ShapeDtypeStruct((slots, hidden), bf16),
             jax.ShapeDtypeStruct((slots, hidden), bf16),
         ),
-        in_specs=[in_vmem, in_vmem] + [anywhere] * 5,
-        out_specs=(in_vmem, anywhere, anywhere, anywhere),
+        in_specs=[anywhere, in_vmem] + [anywhere] * 5,
+        out_specs=(anywhere, anywhere, anywhere, anywhere),
         scratch_shapes=[
+            pltpu.VMEM((token_count, model_width), bf16),
+            pltpu.VMEM((groups, capacity, model_width), bf16),
             pltpu.VMEM((chunks, width, hidden), bf16),
             pltpu.VMEM((chunks, width, hidden), bf16),
             pltpu.VMEM((3, slots, hidden), bf16),
@@ -397,8 +441,8 @@
             pltpu.VMEM((chunks, 2, 2, rows // 2, width), bf16),
             pltpu.VMEM((chunks, rows, width), bf16),
             pltpu.VMEM((chunks, rows, width), bf16),
-            pltpu.SemaphoreType.DMA((2 * chunks + 3,)),
-            pltpu.SemaphoreType.DMA((chunks + 2,)),
+            pltpu.SemaphoreType.DMA((2 * chunks + 4,)),
+            pltpu.SemaphoreType.DMA((2 * chunks + 2,)),
             pltpu.SemaphoreType.DMA((chunks,)),
             pltpu.SemaphoreType.DMA((chunks, COPIES)),
             pltpu.SemaphoreType.DMA((chunks, COPIES)),
@@ -406,24 +450,28 @@
         compiler_params=pltpu.CompilerParams(
             collective_id=0, has_side_effects=True, vmem_limit_bytes=60 * 1024 * 1024
         ),
-    )(outgoing, selection, weight_gate, weight_up, gate_pre, up_pre, hidden_grad)
-    tile = min(512, model_width)
+    )(tokens, expert_ids, weight_gate, weight_up, gate_pre, up_pre, hidden_grad)
+    tile = min(1024, model_width)
     wgrad_shape = jax.ShapeDtypeStruct((1, model_width, hidden), jnp.float32)
-    gate_wgrad, up_wgrad = pl.pallas_call(
-        weight_grad_kernel,
+    token_grad, gate_wgrad, up_wgrad = pl.pallas_call(
+        functools.partial(weight_grad_kernel, groups, capacity),
         grid=(model_width // tile,),
-        out_shape=(wgrad_shape, wgrad_shape),
+        out_shape=(jax.ShapeDtypeStruct((token_count, model_width), bf16), wgrad_shape, wgrad_shape),
         in_specs=[
+            pl.BlockSpec(expert_ids.shape, lambda i: (0, 0)),
+            pl.BlockSpec((rows, tile), lambda i: (0, i)),
             pl.BlockSpec((slots, tile), lambda i: (0, i)),
             pl.BlockSpec((slots, hidden), lambda i: (0, 0)),
             pl.BlockSpec((slots, hidden), lambda i: (0, 0)),
         ],
         out_specs=(
+            pl.BlockSpec((token_count, tile), lambda i: (0, i)),
             pl.BlockSpec((1, tile, hidden), lambda i: (0, i, 0)),
             pl.BlockSpec((1, tile, hidden), lambda i: (0, i, 0)),
         ),
-        compiler_params=pltpu.CompilerParams(vmem_limit_bytes=48 * 1024 * 1024),
-    )(block_rows, gate_rows, up_rows)
+        scratch_shapes=[pltpu.VMEM((token_count, rows), bf16)],
+        compiler_params=pltpu.CompilerParams(vmem_limit_bytes=63 * 1024 * 1024),
+    )(expert_ids, returned, block_rows, gate_rows, up_rows)
     return (token_grad, gate_wgrad, up_wgrad)
 
 

time: 79 us -> 71.7 us (0.908)
  local copies, waits for them, and re-layouts: 5.77 us -> 1.35 us
  other arithmetic: 1.09 us -> 0 us
  matrix products: 1.07 us -> 0 us
    unnamed x8 -> x1, local copies, waits for them, and re-layouts: 4.82 us -> 1.35 us
    pallas_call x1, Pallas kernels: 56.5 us -> 54.8 us  [on_device(): pl.pallas_call(functools.partial(exchange_kernel, groups, capacity, chunk...]
    pallas_call x1, Pallas kernels: 13.4 us -> 14.7 us  [on_device(): pl.pallas_call(functools.partial(weight_grad_kernel, groups, capacity), g...]
    dot_general x1 -> x0, matrix products: 1.07 us -> none  [rows_inner(): lax.dot_general(left_rows, right_rows, (((0,), (0,)), ((), ())), preferre...]
    convert_element_type x4 -> x0, other arithmetic: 0.81 us -> none  [the longest x2 0.8 us: slot_table(): one_hot = (expert_ids[:, :, None] == labels).astype(jnp.int32)]
where the time goes in v2:
time: 71.7 us; the launch traced here: 71.5 us
  Pallas kernels  69.5 us (97%)
  local copies, waits for them, and re-layouts  1.35 us (2%)
    pallas_call x1, Pallas kernels, on_device(): pl.pallas_call(functools.partial(exchange_kernel, groups, capacity, chunk...  54.8 us
    pallas_call x1, Pallas kernels, on_device(): pl.pallas_call(functools.partial(weight_grad_kernel, groups, capacity), g...  14.7 us

profile of v2, /device:TPU:0, one launch (start us, length us, event | category | flops | bytes accessed | tf_op | source)
XLA Modules:
  0.0 71.5 jit_solution(4790408322568186875)
XLA Ops:
  0.6 1.4 %copy.11.expert_ids = s32[24,2]{1,0:T(8,128)} copy(s32[24,2]{0,1:T(2,128)} %param.8) | data formatting | bytes 384 | tf_op args[1]
  2.0 54.8 %shard_map.94 = (bf16[64,4096]{1,0:T(8,128)(2,1)}, bf16[512,4096]{1,0:T(8,128)(2,1)}, bf16[512,1024]{1,0:T(8,128)(2,1)}, bf16[512,1024]{1,0:T(8,128)(2,1)}) custom-call(bf16[24,4096]{1,0:T(8,128)(2,1)} %tokens.1, s32[24,2]{1,0:T(8,128)} %copy.11.expert_ids, bf16[1,4096,1024]{2,1,0:T(8,128)(2,1)} %weight_gate.1, bf16[1,4096,1024]{2,1,0:T(8,128)(2,1)} %weight_up.1, ...), custom_call_target="tpu_custom_call" | custom-call | tf_op jit(solution)/shard_map/pallas_call | solution.py:418
  56.8 14.7 %shard_map.95 = (bf16[24,4096]{1,0:T(8,128)(2,1)}, f32[1,4096,1024]{2,1,0:T(8,128)}, f32[1,4096,1024]{2,1,0:T(8,128)}) custom-call(s32[24,2]{1,0:T(8,128)} %copy.11.expert_ids, bf16[64,4096]{1,0:T(8,128)(2,1)} %get-tuple-element.7.returned, bf16[512,4096]{1,0:T(8,128)(2,1)} %get-tuple-element.8.block_rows, bf16[512,1024]{1,0:T(8,128)(2,1)} %get-tuple-element.9.gate_rows, ...), custom_call_target="tpu_custom_call" | custom-call | tf_op jit(solution)/shard_map/pallas_call | solution.py:456
